TPU v7x, 32 devices: a 4x4x1 block of a 4x4x8 slice. The times are simulated.
32 devices in a mesh: dp: 1 (over z), tp: 32 (over y, x, core).
Axes of the slice: x: 4, y: 4, z: 1, core: 2. Of those that a mesh axis runs over, the one named last changes fastest.
The devices are a block of a 4x4x8 slice.
Arguments:
- hidden: bfloat16 [1536, 896], P(('dp', 'tp'))
- ln_gamma: float32 [896], replicated
- ln_beta: float32 [896], replicated
- out_embed: bfloat16 [155648, 896], P('tp')
- vocab_valid: int32 [155648], P('tp')
- targets: int32 [1536], P(('dp', 'tp'))
- loss_mask: int32 [1536], P(('dp', 'tp'))
Outputs:
- output 1: float32 [1536], P(('dp', 'tp'))
- output 2: float32 [1], P('dp')
- output 3: bfloat16 [1536, 896], P(('dp', 'tp'))
- output 4: float32 [155648, 896], P(('dp', 'tp'))
- output 5: float32 [896], P('dp')
- output 6: float32 [896], P('dp')
All inputs are finite; a program needn't handle non-finite values.
Results may differ from a plain program's by a relative error of at most 0.001.
Values are sent between devices in bfloat16 or wider.
A program may use at most 768 MiB of HBM per device.

v0:
```python
import jax
import jax.numpy as jnp
from jax import lax
from jax.sharding import PartitionSpec as P

LN_EPS = 1e-5


def layer_norm(hidden32, ln_gamma, ln_beta):
    row_mean = jnp.mean(hidden32, axis=-1, keepdims=True)
    centered = hidden32 - row_mean
    row_var = jnp.mean(centered * centered, axis=-1, keepdims=True)
    return centered * lax.rsqrt(row_var + LN_EPS) * ln_gamma + ln_beta


def solution(mesh):
    tok_spec = P(("dp", "tp"))
    row_spec = P(("dp", "tp"), None)

    def local_step(hidden_blk, ln_gamma, ln_beta, embed_blk, valid_blk, tgt_blk, mask_blk):
        tok_local = hidden_blk.shape[0]
        shard_vocab = embed_blk.shape[0]
        shard_idx = lax.axis_index("tp")
        normed, ln_vjp = jax.vjp(layer_norm, hidden_blk.astype(jnp.float32), ln_gamma, ln_beta)
        x_all = lax.all_gather(normed.astype(jnp.bfloat16), "tp", axis=0, tiled=True)
        labels = lax.all_gather(jnp.stack([tgt_blk, mask_blk]), "tp", axis=1, tiled=True)
        weight = labels[1].astype(jnp.float32)
        logits = lax.dot_general(x_all, embed_blk, (((1,), (1,)), ((), ())), preferred_element_type=jnp.float32)
        allowed = (valid_blk > 0)[None, :]
        local_max = jnp.max(jnp.where(allowed, logits, -jnp.inf), axis=1)
        row_max = lax.pmax(local_max, "tp")
        shifted_exp = jnp.where(allowed, jnp.exp(logits - row_max[:, None]), 0.0)
        target_hit = (jnp.arange(shard_vocab) + shard_idx * shard_vocab)[None, :] == labels[0][:, None]
        picked_part = jnp.sum(jnp.where(target_hit, logits, 0.0), axis=1)
        tok_stats = lax.psum(jnp.stack([jnp.sum(shifted_exp, axis=1), picked_part]), "tp")
        log_norm = row_max + jnp.log(tok_stats[0])
        tok_count = jnp.sum(weight)
        tok_loss = (log_norm - tok_stats[1]) * weight
        mean_loss = (jnp.sum(tok_loss) / tok_count).reshape(1)
        soft_probs = shifted_exp / tok_stats[0][:, None]
        d_logits = ((soft_probs - target_hit.astype(jnp.float32)) * (weight / tok_count)[:, None]).astype(jnp.bfloat16)
        d_embed = lax.dot_general(d_logits, x_all, (((0,), (0,)), ((), ())), preferred_element_type=jnp.float32)
        dx_part = jnp.dot(d_logits, embed_blk, preferred_element_type=jnp.float32)
        dx_local = lax.psum_scatter(dx_part, "tp", scatter_dimension=0, tiled=True)
        d_hidden, d_gamma, d_beta = ln_vjp(dx_local)
        ln_grads = lax.psum(jnp.stack([d_gamma, d_beta]), "tp")
        loss_local = lax.dynamic_slice_in_dim(tok_loss, shard_idx * tok_local, tok_local)
        return loss_local, mean_loss, d_hidden.astype(jnp.bfloat16), d_embed, ln_grads[0], ln_grads[1]

    return jax.shard_map(local_step, mesh=mesh, in_specs=(row_spec, P(), P(), P("tp", None), P("tp"), tok_spec, tok_spec), out_specs=(tok_spec, P("dp"), row_spec, row_spec, P("dp"), P("dp")), check_vma=False)
```

profile of v0, /device:TPU:97, one launch (start us, length us, event | category | flops | bytes accessed | tf_op | source)
XLA Modules:
  0.0 357.7 jit_solution(13255318105519340178)
XLA Ops:
  7.2 0.1 all-gather.3.cloned.1.call-start
  7.2 1.0 convert_reduce_fusion
  8.3 1.1 fusion.14
  9.4 1.6 fusion.12
  11.0 0.1 all-gather.3.cloned.1.call-update
  11.1 0.1 reduce-scatter.2.cloned.1.call-start
  11.1 0.7 add_bitcast_fusion
  11.8 32.1 %all-gather = s32[32,48,2]{1,2,0:T(2,128)S(1)} all-gather(s32[1,48,2]{1,2,0:T(2,128)S(1)} %add_bitcast_fusion), channel_id=1, replica_groups=mesh['dp'=1,'tp'=32] {'tp'}, dimensions={0}, use_global_device_ids=true | all-gather | bytes 12672 | tf_op jit(solution)/shard_map/all_gather | solution.py:26
  43.9 0.1 reshape.70
  44.1 0.6 fusion.16
  44.7 0.7 broadcast_compare_fusion
  45.4 9.3 %all-gather.3.cloned.1.call-done = bf16[1536,896]{1,0:T(8,128)(2,1)} async-done(((bf16[48,896]{1,0:T(8,128)(2,1)}), bf16[1536,896]{1,0:T(8,128)(2,1)}) %all-gather.3.cloned.1.call-update) | async-done | bytes 2752528 | tf_op jit(solution)/shard_map/all_gather | solution.py:25
  54.7 23.7 %select_reduce_fusion = (f32[1536]{0:T(1024)S(1)}, f32[1536,4864]{1,0:T(8,128)}) fusion(pred[4864]{0:T(1024)(128)(4,1)S(1)} %broadcast_compare_fusion, bf16[1536,896]{1,0:T(8,128)(2,1)} %all-gather.3.cloned.1.call-done, bf16[4864,896]{1,0:T(8,128)(2,1)} %param.10), kind=kOutput, calls=%fused_computation.7 | convolution fusion | flops 13403158528 | bytes 41364224 | tf_op jit(solution)/shard_map/dot_general | solution.py:28
  78.4 44.4 %pmax.7 = f32[1536]{0:T(1024)S(1)} all-reduce(f32[1536]{0:T(1024)S(1)} %get-tuple-element.22), channel_id=1, replica_groups=mesh['dp'=1,'tp'=32] {'tp'}, use_global_device_ids=true, to_apply=%region_3.4 | all-reduce | flops 1536 | bytes 12288 | tf_op jit(solution)/shard_map/pmax | solution.py:31
  122.8 15.1 %fusion.4 = (f32[1536]{0:T(1024)S(1)}, f32[1536]{0:T(1024)S(1)}) fusion(f32[1536,4864]{1,0:T(8,128)} %get-tuple-element.23, f32[1536]{0:T(1024)S(1)} %pmax.7, pred[4864]{0:T(1024)(128)(4,1)S(1)} %broadcast_compare_fusion, s32[1536]{0:T(1024)S(1)} %slice_reduce_fusion.2, s32[4864]{0:T(1024)S(1)} %iota_add_fusion), kind=kLoop, calls=%fused_computation.8 | loop fusion | flops 44823552 | bytes 29933312 | tf_op jit(solution)/shard_map/reduce_sum | solution.py:35
  138.0 45.0 %psum.14 = f32[2,1536]{1,0:T(2,128)S(1)} all-reduce(f32[2,1536]{1,0:T(2,128)S(1)} %pad_maximum_fusion), channel_id=1, replica_groups=mesh['dp'=1,'tp'=32] {'tp'}, use_global_device_ids=true, to_apply=%region_6.7 | all-reduce | flops 3072 | bytes 24576 | tf_op jit(solution)/shard_map/psum | solution.py:35
  183.0 1.3 fusion.20
  184.2 16.0 %fusion.3 = bf16[1536,4864]{1,0:T(8,128)(2,1)S(1)} fusion(f32[1536,4864]{1,0:T(8,128)} %get-tuple-element.23, f32[1536]{0:T(1024)S(1)} %get-tuple-element.21, f32[1536]{0:T(1024)S(1)} %get-tuple-element.13, s32[4864]{0:T(1024)S(1)} %iota_add_fusion, f32[1536]{0:T(1024)S(1)} %pmax.7, s32[1536]{0:T(1024)S(1)} %slice_reduce_fusion.2, ...), kind=kLoop, calls=%fused_computation.5 | loop fusion | flops 59768832 | bytes 44875520 | tf_op jit(solution)/shard_map/convert_element_type | solution.py:41
  200.3 0.0 copy-start
  200.3 5.3 %copy-done = bf16[1536,4864]{1,0:T(8,128)(2,1)} copy-done((bf16[1536,4864]{1,0:T(8,128)(2,1)}, bf16[1536,4864]{1,0:T(8,128)(2,1)S(1)}, u32[]{:S(2)}) %copy-start) | copy-done | bytes 14942232
  205.5 0.0 copy-start.3
  205.5 19.7 %fusion.21 = f32[1536,896]{1,0:T(8,128)} fusion(bf16[1536,4864]{1,0:T(8,128)(2,1)S(1)} %fusion.3, bf16[4864,896]{1,0:T(8,128)(2,1)} %param.10), kind=kOutput, calls=%fused_computation.46 | convolution fusion | flops 13388218368 | bytes 29163520 | tf_op jit(solution)/shard_map/dot_general | solution.py:43
  225.3 0.1 reduce-scatter.2.cloned.1.call-update
  226.7 0.6 dynamic_slice.3
  227.3 0.0 copy-done.3
  227.3 0.0 copy-start.1
  227.3 0.0 copy-start.2
  227.3 21.6 %fusion.22 = f32[4864,896]{1,0:T(8,128)} fusion(bf16[1536,4864]{1,0:T(8,128)(2,1)} %copy-done, bf16[1536,896]{1,0:T(8,128)(2,1)S(1)} %copy-done.3), kind=kOutput, calls=%fused_computation.47 | convolution fusion | flops 13388218368 | bytes 35127296 | tf_op jit(solution)/shard_map/dot_general | solution.py:42
  248.9 50.7 %reduce-scatter.2.cloned.1.call-done = f32[48,896]{1,0:T(8,128)} async-done(((f32[1536,896]{1,0:T(8,128)}), f32[48,896]{1,0:T(8,128)}) %reduce-scatter.2.cloned.1.call-update) | async-done | bytes 172048 | tf_op jit(solution)/shard_map/reduce_scatter | solution.py:44
  299.6 0.0 copy-done.1
  299.6 0.0 copy-done.2
  299.6 1.1 fusion.13
  300.8 1.1 fusion.19
  302.0 46.4 %psum.15 = f32[2,896]{1,0:T(2,128)S(1)} all-reduce(f32[2,896]{1,0:T(2,128)S(1)} %pad_maximum_fusion.1), channel_id=1, replica_groups=mesh['dp'=1,'tp'=32] {'tp'}, use_global_device_ids=true, to_apply=%region_14.15 | all-reduce | flops 1792 | bytes 14336 | tf_op jit(solution)/shard_map/psum | solution.py:46
  348.4 0.6 slice_reduce_fusion.3
  349.0 0.7 add_convert_fusion
  (14 shorter events, 0.1 us)
Async XLA Ops:
  7.2 47.5 %all-gather.3.cloned.1.call-start = ((), (), s32[]{:S(2)}) async-start(), calls=%async_computation.1 | async-start | bytes 2838528 | tf_op jit(solution)/shard_map/all_gather | solution.py:25
  11.1 288.6 %reduce-scatter.2.cloned.1.call-start = ((), (), s32[]{:S(2)}) async-start(), calls=%async_computation.2 | async-start | bytes 5677056 | tf_op jit(solution)/shard_map/reduce_scatter | solution.py:44
  200.3 5.3 %copy-start = (bf16[1536,4864]{1,0:T(8,128)(2,1)}, bf16[1536,4864]{1,0:T(8,128)(2,1)S(1)}, u32[]{:S(2)}) copy-start(bf16[1536,4864]{1,0:T(8,128)(2,1)S(1)} %fusion.3) | copy-start | bytes 44826628
  205.5 21.7 %copy-start.3 = (bf16[1536,896]{1,0:T(8,128)(2,1)S(1)}, bf16[1536,896]{1,0:T(8,128)(2,1)}, u32[]{:S(2)}) copy-start(bf16[1536,896]{1,0:T(8,128)(2,1)} %all-gather.3.cloned.1.call-done) | copy-start | bytes 8257540
  227.3 72.4 %copy-start.1 = (bf16[48,896]{1,0:T(8,128)(2,1)S(1)}, bf16[48,896]{1,0:T(8,128)(2,1)}, u32[]{:S(2)}) copy-start(bf16[48,896]{1,0:T(8,128)(2,1)} %param.7) | copy-start | bytes 258052
  227.3 72.4 %copy-start.2 = (f32[896]{0:T(1024)S(1)}, f32[896]{0:T(1024)}, u32[]{:S(2)}) copy-start(f32[896]{0:T(1024)} %param.8) | copy-start | bytes 10756
Sparse Core Ops, SparseCore 0:
  11.2 43.4 all-gather.2
  225.5 74.1 reduce-scatter.1
where the time goes:
time: 359 us; the launch traced here: 358 us
  blocking collectives  168 us (47%)
  matrix products  65.1 us (18%)
  waiting for transfers between devices  60.1 us (17%)
  other arithmetic  41.2 us (11%)
  between operations  16.7 us (5%)
  local copies, waits for them, and re-layouts  6.64 us (2%)
    reduce_scatter x1, waiting for transfers between devices, local_step(): dx_local = lax.psum_scatter(dx_part, 'tp', scatter_dimension=0, tiled=True)  50.7 us
    psum x1, blocking collectives, local_step(): ln_grads = lax.psum(jnp.stack([d_gamma, d_beta]), 'tp')  46.4 us
    psum x1, blocking collectives, local_step(): lax.psum(jnp.stack([jnp.sum(shifted_exp, axis=1), picked_part]), 'tp')  45 us
    pmax x1, blocking collectives, local_step(): row_max = lax.pmax(local_max, 'tp')  44.4 us
    all_gather x1, blocking collectives, local_step(): lax.all_gather(jnp.stack([tgt_blk, mask_blk]), 'tp', axis=1, tiled=True)  32.1 us
    dot_general x1, matrix products, local_step(): lax.dot_general(x_all, embed_blk, (((1,), (1,)), ((), ())), preferred_ele...  23.7 us
    dot_general x1, matrix products, local_step(): lax.dot_general(d_logits, x_all, (((0,), (0,)), ((), ())), preferred_elem...  21.6 us
    dot_general x1, matrix products, local_step(): dx_part = jnp.dot(d_logits, embed_blk, preferred_element_type=jnp.float32)  19.7 us
  transfers between devices with their start and end apart: 2, of which 2 were waited for; matrix products, arithmetic and copies ran while one was open for 7% of the time, Pallas kernels for 0%

commit v1 on v0

v1 whole, which is shorter than its diff:
```python
import functools
import math

import jax
import jax.numpy as jnp
from jax import lax
from jax.experimental import pallas as pl
from jax.experimental.pallas import tpu as pltpu
from jax.sharding import PartitionSpec as P

LN_EPS = 1e-5
F32 = jnp.float32
BF16 = jnp.bfloat16
LANES = 128
LOW = -3e38
NN = (((1,), (0,)), ((), ()))
NT = (((1,), (1,)), ((), ()))
TN = (((0,), (0,)), ((), ()))


def dot(a, b, dims):
    return lax.dot_general(a, b, dims, preferred_element_type=F32)


def pieces(lo, hi, size):
    return [(o, min(size, hi - o)) for o in range(lo, hi, size)]


def head_kernel(
    side, tok, dim, vocab,
    hid_ref, gamma_ref, beta_ref, aux_ref, bias_ref, emb_hbm,
    loss_ref, mean_ref, dhid_ref, dln_ref, dz_hbm, x_hbm,
    emb, xbuf, z, tcol, stage, ms, ss, pk, lsec, wcol,
    st, rowa, rowb, mrow, lrow,
    dxt, rca, rcb, rcd, rcc, ga, gb, gpart,
    emb_sem, ag_s, ag_r, sa_s, sa_r, sb_s, sb_r,
    s0_s, s0_r, s1_s, s1_r, s2_s, s2_r, s3_s, s3_r,
    ga_s, ga_r, gb_s, gb_r, dz_sem, x_sem,
):
    n_row = 2 * side
    wide = dim + LANES
    me = lax.axis_index("tp")
    c = lax.rem(me, 2)
    x = lax.rem(me // 2, side)
    y = me // n_row
    off = me * vocab

    def wrap(v):
        return lax.rem(v + 4 * side, side)

    def dev(yy, xx, cc):
        return {"tp": (wrap(yy) * side + wrap(xx)) * 2 + cc}

    right, left = dev(y, x + 1, c), dev(y, x - 1, c)
    up, down = dev(y - 1, x, c), dev(y + 1, x, c)
    partner = dev(y, x, 1 - c)
    row_peers = [(dx, h) for h in range(2) for dx in range(side) if (dx, h) != (0, 0)]

    def other(h):
        return c if h == 0 else 1 - c

    def remote(src, dst, s, r, to):
        return pltpu.make_async_remote_copy(
            src_ref=src, dst_ref=dst, send_sem=s, recv_sem=r,
            device_id=to, device_id_type=pl.DeviceIdType.MESH)

    emb_copy = pltpu.make_async_copy(emb_hbm, emb, emb_sem)
    emb_copy.start()

    barrier = pltpu.get_barrier_semaphore()
    for dx, h in row_peers:
        pl.semaphore_signal(barrier, inc=1, device_id=dev(y, x + dx, other(h)),
                            device_id_type=pl.DeviceIdType.MESH)
    for dy in range(1, side):
        pl.semaphore_signal(barrier, inc=1, device_id=dev(y + dy, x, c),
                            device_id_type=pl.DeviceIdType.MESH)

    def normed():
        h32 = hid_ref[...].astype(F32)
        cen = h32 - jnp.mean(h32, axis=-1, keepdims=True)
        rstd = lax.rsqrt(jnp.mean(cen * cen, axis=-1, keepdims=True) + LN_EPS)
        return cen * rstd, rstd

    xhat0, _ = normed()
    xbuf[0, :, 0:dim] = (xhat0 * gamma_ref[...] + beta_ref[...]).astype(BF16)
    xbuf[0, :, dim:wide] = aux_ref[...]
    pl.semaphore_wait(barrier, len(row_peers) + side - 1)

    cut = 2 * tok // 3
    lo, hi = pl.ds(0, cut), pl.ds(cut, tok - cut)
    ag_ops = {}

    def ag(k, src, dst, to, rows=None):
        a, b = xbuf.at[src], xbuf.at[dst]
        if rows is not None:
            a, b = xbuf.at[src, rows], xbuf.at[dst, rows]
        ag_ops[k] = remote(a, b, ag_s.at[k], ag_r.at[k], to)
        ag_ops[k].start()

    ag(0, 0, 3, right)
    ag(1, 0, 1, left)
    ag(2, 0, 4, partner)
    ag(3, 0, 8, up)
    ag(4, 0, 24, down)
    ag_ops[0].wait_recv()
    ag(5, 3, 2, right, lo)
    ag(7, 3, 7, partner)
    ag(9, 3, 11, up)
    ag(10, 3, 27, down)
    ag_ops[1].wait_recv()
    ag(6, 1, 2, left, hi)
    ag(8, 1, 5, partner)
    ag(11, 1, 9, up)
    ag(12, 1, 25, down)
    ag_ops[5].wait_recv()
    ag_ops[6].wait_recv()
    ag(13, 2, 6, partner)
    ag(14, 2, 10, up)
    ag(15, 2, 26, down)
    for k in (2, 7, 8, 13):
        ag_ops[k].wait_recv()
    for k, src, dst, to in ((16, (8, 4), (12, 4), partner), (17, (24, 4), (28, 4), partner),
                            (18, (8, 2), (16, 2), up), (19, (26, 2), (18, 2), down),
                            (20, (16, 4), (20, 4), partner)):
        ag_ops[k] = remote(xbuf.at[pl.ds(*src)], xbuf.at[pl.ds(*dst)], ag_s.at[k], ag_r.at[k], to)

    def row_of(t):
        return wrap(y + t)

    def sa_op(t, d):
        dx, h = row_peers[d]
        r = row_of(t)
        return remote(st.at[r, pl.ds(0, 3)], rowa.at[t, 2 * x + c], sa_s.at[t, d], sa_r.at[t, d],
                      dev(y, x + dx, other(h)))

    def sa_wait(t, d):
        dx, h = row_peers[d]
        slot = 2 * wrap(x - dx) + other(h)
        remote(rowa.at[t, slot], rowa.at[t, slot], sa_s.at[t, d], sa_r.at[t, d], partner).wait_recv()

    def sb_op(t, dy):
        r = row_of(t)
        return remote(rowb.at[r, y], rowb.at[r, y], sb_s.at[t, dy], sb_r.at[t, dy], dev(y + dy, x, c))

    def sb_wait(t, dy):
        yy = wrap(y - dy)
        ref = rowb.at[wrap(yy + t), yy]
        remote(ref, ref, sb_s.at[t, dy], sb_r.at[t, dy], partner).wait_recv()

    def merge(parts):
        m = functools.reduce(jnp.maximum, [p[0] for p in parts])
        s = functools.reduce(jnp.add, [p[1] * jnp.exp(p[0] - m) for p in parts])
        return m, s, functools.reduce(jnp.add, [p[2] for p in parts])

    def row_merge(t):
        for d in range(len(row_peers)):
            sa_wait(t, d)
        m, s, q = merge([[rowa[t, i, k] for k in range(3)] for i in range(n_row)])
        r = row_of(t)
        rowb[r, y, 0] = m
        rowb[r, y, 1] = s
        rowb[r, y, 2] = q
        for dy in range(1, side):
            sb_op(t, dy).start()

    half = (vocab // LANES // 2) * LANES
    lane = lax.broadcasted_iota(jnp.int32, (tok, LANES), 1)
    digit = jnp.where(lane == 0, 1.0, jnp.where(lane == 1, 256.0, jnp.where(lane == 2, 65536.0, 0.0)))

    def logits_tile(t, carry):
        @pl.when(t == 1)
        def _():
            ag_ops[16].wait_recv()

        @pl.when(t == 2)
        def _():
            ag_ops[20].wait_recv()

        @pl.when(t == 3)
        def _():
            ag_ops[17].wait_recv()

        base = 8 * t
        for p in range(8):
            code = jnp.sum(xbuf[base + p, :, dim:wide].astype(F32) * digit, axis=1, keepdims=True)
            tcol[base + p] = jnp.broadcast_to(code.astype(jnp.int32) - 1 - off, (tok, LANES))
        ms[...] = jnp.full(ms.shape, LOW, F32)
        ss[...] = jnp.zeros(ss.shape, F32)
        pk[...] = jnp.zeros(pk.shape, F32)

        def do_dot(o, n):
            xt = xbuf[pl.ds(base, 8), :, 0:dim].reshape(8 * tok, dim)
            r = dot(xt, emb[o:o + n, :], NT) + bias_ref[:, o:o + n]
            z[pl.ds(base, 8), :, o:o + n] = r.reshape(8, tok, n)

        def do_stats(o, n):
            for p in range(8):
                m0, tl, q = ms[p], tcol[base + p], pk[p]
                zs = [z[base + p, :, o + i:o + i + LANES] for i in range(0, n, LANES)]
                m1 = functools.reduce(jnp.maximum, zs, m0)
                s = ss[p] * jnp.exp(m0 - m1)
                for i, v in enumerate(zs):
                    s = s + jnp.exp(v - m1)
                    q = q + jnp.where(lane + (o + i * LANES) == tl, v, 0.0)
                ms[p], ss[p], pk[p] = m1, s, q

        def run(lo_, hi_):
            cs = pieces(lo_, hi_, 512)
            do_dot(*cs[0])
            for a, b in zip(cs[1:], cs[:-1]):
                do_dot(*a)
                do_stats(*b)
            do_stats(*cs[-1])

        run(0, half)

        @pl.when(t == 0)
        def _():
            for k in (3, 9, 11, 14):
                ag_ops[k].wait_recv()
            ag_ops[16].start()
            ag_ops[18].start()
            for k in (4, 10, 12, 15):
                ag_ops[k].wait_recv()
            ag_ops[17].start()
            ag_ops[19].start()

        @pl.when(t == 1)
        def _():
            ag_ops[18].wait_recv()
            ag_ops[19].wait_recv()
            ag_ops[20].start()

        @pl.when(t > 0)
        def _():
            row_merge(t - 1)

        run(half, vocab)

        r = row_of(t)
        for p in range(8):
            h, j = p // 4, p % 4
            m1 = jnp.max(ms[p], axis=1, keepdims=True)
            s1 = jnp.sum(ss[p] * jnp.exp(ms[p] - m1), axis=1, keepdims=True)
            q1 = jnp.sum(pk[p], axis=1, keepdims=True)
            live = jnp.where(tcol[base + p] == -1 - off, 0.0, 1.0)
            packed = jnp.where(lane == 0, m1, jnp.where(lane == 1, s1, jnp.where(lane == 2, q1, live)))
            flat = jnp.concatenate([packed, jnp.zeros((LANES - tok, LANES), F32)], axis=0).T
            sub = 2 * wrap(x + j) + other(h)
            for k in range(3):
                st[r, k, pl.ds(sub, 1), :] = flat[k:k + 1, :]
            mrow[r, pl.ds(sub, 1), :] = flat[3:4, :]
        for k in range(3):
            rowa[t, 2 * x + c, k] = st[r, k]
        for d in range(len(row_peers)):
            sa_op(t, d).start()
        return carry

    emb_copy.wait()
    lax.fori_loop(0, side, logits_tile, 0)
    row_merge(side - 1)
    for t in range(side):
        for dy in range(1, side):
            sb_wait(t, dy)

    n_tok = jnp.sum(mrow[...])
    inv_n = 1.0 / n_tok
    total = jnp.zeros((n_row, LANES), F32)
    lanes8 = lax.broadcasted_iota(jnp.int32, (n_row, LANES), 1)
    for r in range(side):
        m, s, q = merge([[rowb[r, i, k] for k in range(3)] for i in range(side)])
        lse = m + jnp.log(s)
        lrow[r] = lse
        tl = jnp.where(lanes8 < tok, (lse - q) * mrow[r], 0.0)
        st[r, 3] = tl
        total = total + tl
    loss_ref[...] = st[y, 3, pl.ds(2 * x + c, 1), :]
    mean_ref[...] = jnp.broadcast_to(jnp.sum(total) / n_tok, (1, LANES))

    def blk(k, p):
        h, j = p // 4, p % 4
        cc = other(h)
        yy = wrap(jnp.where(cc == 0, x + j + k, y + j))
        xx = wrap(jnp.where(cc == 0, x + j, y + j - k))
        pos = 8 * wrap(yy - y) + 4 * h + wrap(xx - x)
        return pos, yy, 2 * xx + cc

    along = c
    nxt = dev(y + along, x + 1 - along, c)
    prv = dev(y - along, x - 1 + along, c)
    top, bot = pl.ds(0, tok // 2), pl.ds(tok // 2, tok - tok // 2)

    def s0(k):
        return remote(dxt.at[k, pl.ds(4, 4)], rca.at[k], s0_s.at[k], s0_r.at[k], partner)

    def s1(k, d):
        src = dxt.at[k, 2, top] if d == 0 else dxt.at[k, 2, bot]
        return remote(src, rcb.at[k, d], s1_s.at[k, d], s1_r.at[k, d], prv if d == 0 else nxt)

    def s2(k, d):
        src = dxt.at[k, 1] if d == 0 else dxt.at[k, 3]
        return remote(src, rcd.at[k, d], s2_s.at[k, d], s2_r.at[k, d], nxt if d == 0 else prv)

    def s3_far(k):
        return wrap(jnp.where(c == 0, x + k - y, y - k - x))

    def s3(k):
        i = s3_far(k)
        to = dev(jnp.where(c == 0, x + k, y), jnp.where(c == 0, x, y - k), c)
        slot = wrap(side - i)
        return remote(dxt.at[k, 0], rcc.at[slot], s3_s.at[k], s3_r.at[slot], to)

    def do_s1(k):
        s0(k).wait_recv()
        for j in range(4):
            dxt[k, j] = dxt[k, j] + rca[k, j]
        s1(k, 0).start()
        s1(k, 1).start()

    def do_s2(k):
        s1(k, 0).wait_recv()
        s1(k, 1).wait_recv()
        n = tok // 2
        dxt[k, 3, 0:n] = dxt[k, 3, 0:n] + rcb[k, 0]
        dxt[k, 1, n:tok] = dxt[k, 1, n:tok] + rcb[k, 1]
        s2(k, 0).start()
        s2(k, 1).start()

    def do_s3(k):
        s2(k, 0).wait_recv()
        s2(k, 1).wait_recv()
        dxt[k, 0] = dxt[k, 0] + rcd[k, 0] + rcd[k, 1]
        i = s3_far(k)

        @pl.when(i != 0)
        def _():
            s3(k).start()

        @pl.when(i == 0)
        def _():
            rcc[0] = dxt[k, 0]

    def dz_out(k):
        return pltpu.make_async_copy(
            stage.at[lax.rem(k, 2)], dz_hbm.at[pl.ds(pl.multiple_of(k * 8 * tok, 8 * tok), 8 * tok)], dz_sem.at[k])

    def x_out(k, p):
        pos, _, _ = blk(k, p)
        return pltpu.make_async_copy(
            xbuf.at[pos, :, pl.ds(0, dim)],
            x_hbm.at[pl.ds(pl.multiple_of((8 * k + p) * tok, 16), tok)], x_sem.at[8 * k + p])

    def grad_tile(k, carry):
        where = [blk(k, p) for p in range(8)]
        for p, (pos, yy, sub) in enumerate(where):
            row = lrow[yy, pl.ds(sub, 1), :]
            lsec[p] = jnp.broadcast_to(row, (LANES, LANES)).T[0:tok, :]
            wcol[p] = jnp.where(tcol[pos] == -1 - off, 0.0, inv_n)
            x_out(k, p).start()
        buf = lax.rem(k, 2)

        @pl.when(k >= 2)
        def _():
            dz_out(k - 2).wait()

        def part(o, n):
            rows = []
            for p, (pos, _, _) in enumerate(where):
                l, w, tl = lsec[p], wcol[p], tcol[pos]
                cols = []
                for i in range(o, o + n, LANES):
                    e = jnp.exp(z[pos, :, i:i + LANES] - l)
                    e = jnp.where(lane + i == tl, e - 1.0, e) * w
                    cols.append(e.astype(BF16))
                rows.append(jnp.concatenate(cols, axis=1))
            dz = jnp.concatenate(rows, axis=0)
            stage[buf, :, o:o + n] = dz
            return dot(dz, emb[o:o + n, :], NN)

        def span(lo_, hi_):
            return functools.reduce(jnp.add, [part(o, n) for o, n in pieces(lo_, hi_, 512)])

        dxt[k] = span(0, half).reshape(8, tok, dim)

        @pl.when(k >= 1)
        def _():
            do_s1(k - 1)

        @pl.when(k >= 2)
        def _():
            do_s2(k - 2)

        @pl.when(k >= 3)
        def _():
            do_s3(k - 3)

        dxt[k] = dxt[k] + span(half, vocab).reshape(8, tok, dim)
        s0(k).start()
        dz_out(k).start()
        return carry

    lax.fori_loop(0, side, grad_tile, 0)
    last = side - 1
    do_s1(last)
    do_s2(last - 1)
    do_s3(last - 2)
    do_s2(last)
    do_s3(last - 1)
    do_s3(last)
    for i in range(1, side):
        ref = rcc.at[i]
        remote(ref, ref, s3_s.at[0], s3_r.at[i], partner).wait_recv()

    dx = rcc[0] + rcc[1] + rcc[2] + rcc[3]
    xhat, rstd = normed()
    g = dx * gamma_ref[...]
    dh = rstd * (g - jnp.mean(g, axis=-1, keepdims=True) - xhat * jnp.mean(g * xhat, axis=-1, keepdims=True))
    gpart[0:1, :] = jnp.sum(dx * xhat, axis=0, keepdims=True)
    gpart[1:2, :] = jnp.sum(dx, axis=0, keepdims=True)

    def ga_op(d):
        ddx, h = row_peers[d]
        return remote(gpart, ga.at[2 * x + c], ga_s.at[d], ga_r.at[d], dev(y, x + ddx, other(h)))

    def gb_op(dy):
        return remote(gb.at[y], gb.at[y], gb_s.at[dy], gb_r.at[dy], dev(y + dy, x, c))

    for d in range(len(row_peers)):
        ga_op(d).start()
    dhid_ref[...] = dh.astype(BF16)
    ga[2 * x + c] = gpart[...]
    for d, (ddx, h) in enumerate(row_peers):
        ref = ga.at[2 * wrap(x - ddx) + other(h)]
        remote(ref, ref, ga_s.at[d], ga_r.at[d], partner).wait_recv()
    gb[y] = functools.reduce(jnp.add, [ga[i] for i in range(n_row)])
    for dy in range(1, side):
        gb_op(dy).start()
    for dy in range(1, side):
        ref = gb.at[wrap(y - dy)]
        remote(ref, ref, gb_s.at[dy], gb_r.at[dy], partner).wait_recv()
    dln_ref[...] = functools.reduce(jnp.add, [gb[i] for i in range(side)])

    for k in sorted(ag_ops):
        ag_ops[k].wait_send()
    for t in range(side):
        for d in range(len(row_peers)):
            sa_op(t, d).wait_send()
        for dy in range(1, side):
            sb_op(t, dy).wait_send()
        s0(t).wait_send()
        for d in range(2):
            s1(t, d).wait_send()
            s2(t, d).wait_send()

        @pl.when(s3_far(t) != 0)
        def _():
            s3(t).wait_send()

        for p in range(8):
            x_out(t, p).wait()
    for d in range(len(row_peers)):
        ga_op(d).wait_send()
    for dy in range(1, side):
        gb_op(dy).wait_send()
    dz_out(side - 2).wait()
    dz_out(side - 1).wait()


def head(mesh, hid, gamma, beta, aux, bias, emb):
    n_dev = mesh.shape["tp"]
    side = math.isqrt(n_dev // 2)
    tok, dim = hid.shape
    vocab = emb.shape[0]
    seq = tok * n_dev
    n_row = 2 * side
    vmem = pl.BlockSpec(memory_space=pltpu.VMEM)
    hbm = pl.BlockSpec(memory_space=pl.ANY)
    dma = pltpu.SemaphoreType.DMA
    return pl.pallas_call(
        functools.partial(head_kernel, side, tok, dim, vocab),
        out_shape=(
            jax.ShapeDtypeStruct((1, LANES), F32),
            jax.ShapeDtypeStruct((1, LANES), F32),
            jax.ShapeDtypeStruct((tok, dim), BF16),
            jax.ShapeDtypeStruct((2, dim), F32),
            jax.ShapeDtypeStruct((seq, vocab), BF16),
            jax.ShapeDtypeStruct((seq, dim), BF16),
        ),
        in_specs=[vmem] * 5 + [hbm],
        out_specs=(vmem, vmem, vmem, vmem, hbm, hbm),
        scratch_shapes=[
            pltpu.VMEM((vocab, dim), BF16),
            pltpu.VMEM((n_dev, tok, dim + LANES), BF16),
            pltpu.VMEM((n_dev, tok, vocab), F32),
            pltpu.VMEM((n_dev, tok, LANES), jnp.int32),
            pltpu.VMEM((2, 8 * tok, vocab), BF16),
            pltpu.VMEM((8, tok, LANES), F32),
            pltpu.VMEM((8, tok, LANES), F32),
            pltpu.VMEM((8, tok, LANES), F32),
            pltpu.VMEM((8, tok, LANES), F32),
            pltpu.VMEM((8, tok, LANES), F32),
            pltpu.VMEM((side, 4, n_row, LANES), F32),
            pltpu.VMEM((side, n_row, 3, n_row, LANES), F32),
            pltpu.VMEM((side, side, 3, n_row, LANES), F32),
            pltpu.VMEM((side, n_row, LANES), F32),
            pltpu.VMEM((side, n_row, LANES), F32),
            pltpu.VMEM((side, 8, tok, dim), F32),
            pltpu.VMEM((side, 4, tok, dim), F32),
            pltpu.VMEM((side, 2, tok // 2, dim), F32),
            pltpu.VMEM((side, 2, tok, dim), F32),
            pltpu.VMEM((side, tok, dim), F32),
            pltpu.VMEM((n_row, 2, dim), F32),
            pltpu.VMEM((side, 2, dim), F32),
            pltpu.VMEM((2, dim), F32),
            dma,
            dma((21,)), dma((21,)),
            dma((side, n_row - 1)), dma((side, n_row - 1)),
            dma((side, side)), dma((side, side)),
            dma((side,)), dma((side,)),
            dma((side, 2)), dma((side, 2)),
            dma((side, 2)), dma((side, 2)),
            dma((side,)), dma((side,)),
            dma((n_row - 1,)), dma((n_row - 1,)),
            dma((side,)), dma((side,)),
            dma((side,)), dma((n_dev,)),
        ],
        compiler_params=pltpu.CompilerParams(
            collective_id=0, has_side_effects=True, vmem_limit_bytes=67043328),
        name="head",
    )(hid, gamma, beta, aux, bias, emb)


def dembed_kernel(x_ref, dz_ref, out_ref):
    out_ref[...] = dot(dz_ref[...], x_ref[...], TN)


def dembed(x, dz):
    seq, dim = x.shape
    vocab = dz.shape[1]
    cols = 1664
    return pl.pallas_call(
        dembed_kernel,
        out_shape=jax.ShapeDtypeStruct((vocab, dim), F32),
        grid=(pl.cdiv(vocab, cols),),
        in_specs=[pl.BlockSpec((seq, dim), lambda i: (0, 0)), pl.BlockSpec((seq, cols), lambda i: (0, i))],
        out_specs=pl.BlockSpec((cols, dim), lambda i: (i, 0)),
        compiler_params=pltpu.CompilerParams(vmem_limit_bytes=67043328),
        name="dembed",
    )(x, dz)


def solution(mesh):
    tok_spec = P(("dp", "tp"))
    row_spec = P(("dp", "tp"), None)

    def local_step(hidden_blk, ln_gamma, ln_beta, embed_blk, valid_blk, tgt_blk, mask_blk):
        tok = hidden_blk.shape[0]
        code = jnp.where(mask_blk > 0, tgt_blk + 1, 0)
        lane = lax.broadcasted_iota(jnp.int32, (tok, LANES), 1)
        aux = jnp.where(lane < 3, (code[:, None] >> (8 * jnp.minimum(lane, 2))) & 255, 0).astype(BF16)
        bias = jnp.where(valid_blk > 0, 0.0, -jnp.inf).astype(F32)[None, :]
        loss, mean, dhid, dln, dz, x = head(
            mesh, hidden_blk, ln_gamma[None, :], ln_beta[None, :], aux, bias, embed_blk)
        d_embed = dembed(x, dz)
        return loss[0, :tok], mean[0, :1], dhid, d_embed, dln[0], dln[1]

    return jax.shard_map(
        local_step, mesh=mesh,
        in_specs=(row_spec, P(), P(), P("tp", None), P("tp"), tok_spec, tok_spec),
        out_specs=(tok_spec, P("dp"), row_spec, row_spec, P("dp"), P("dp")), check_vma=False)
```

time: 359 us -> 133 us (0.37)
  blocking collectives: 168 us -> 0 us
  Pallas kernels: 0 us -> 121 us
  matrix products: 65.1 us -> 0 us
  waiting for transfers between devices: 60.1 us -> 0 us
  other arithmetic: 41.2 us -> 2.09 us
  between operations: 16.7 us -> 2.34 us
    pallas_call x0 -> x2, Pallas kernels: none -> 121 us  [the longest x1 98.8 us: head(): pl.pallas_call(functools.partial(head_kernel, side, tok, dim, vocab), out...]
    psum x2 -> x0, blocking collectives: 91.4 us -> none  [the longest x1 46.4 us: local_step(): ln_grads = lax.psum(jnp.stack([d_gamma, d_beta]), 'tp')]
    dot_general x3 -> x0, matrix products: 65.1 us -> none  [the longest x1 23.7 us: local_step(): lax.dot_general(x_all, embed_blk, (((1,), (1,)), ((), ())), preferred_ele...]
    reduce_scatter x1 -> x0, waiting for transfers between devices: 50.7 us -> none  [local_step(): dx_local = lax.psum_scatter(dx_part, 'tp', scatter_dimension=0, tiled=True)]
    pmax x1 -> x0, blocking collectives: 44.4 us -> none  [local_step(): row_max = lax.pmax(local_max, 'tp')]
    all_gather x1 -> x0, blocking collectives: 32.1 us -> none  [local_step(): lax.all_gather(jnp.stack([tgt_blk, mask_blk]), 'tp', axis=1, tiled=True)]
    reduce_sum x7 -> x0, other arithmetic: 21.3 us -> none  [the longest x1 15.1 us: local_step(): jnp.sum(shifted_exp, axis=1)]
    convert_element_type x3 -> x1, other arithmetic: 18.4 us -> 0.68 us  [local_step(): jnp.where(lane < 3, code[:, None] >> 8 * jnp.minimum(lane, 2) & 255, 0)]
  transfers between devices with their start and end apart: 2 -> 0, of which waited for: 2 -> 0; matrix products, arithmetic and copies ran while one was open for 7% -> 0% of each run, Pallas kernels for 0% -> 0%
where the time goes in v1:
time: 133 us
  Pallas kernels  121 us (91%)
  local copies, waits for them, and re-layouts  7.19 us (5%)
  between operations  2.34 us (2%)
  other arithmetic  2.09 us (2%)
    pallas_call x1, Pallas kernels, head(): pl.pallas_call(functools.partial(head_kernel, side, tok, dim, vocab), out...  98.8 us
    pallas_call x1, Pallas kernels, dembed(): pl.pallas_call(dembed_kernel, out_shape=jax.ShapeDtypeStruct((vocab, dim)...  22.4 us

profile of v1, /device:TPU:97, one launch (start us, length us, event | category | flops | bytes accessed | tf_op | source)
XLA Modules:
  0.0 132.8 jit_solution(13638217976776277008)
XLA Ops:
  0.6 0.7 compare_select_fusion
  1.4 0.6 broadcast_in_dim.29.bias_ref
  2.0 0.7 compare_select_fusion.1
  2.7 0.7 select_convert_fusion.aux_ref
  3.3 1.3 broadcast_in_dim.24.gamma_ref
  4.6 1.3 broadcast_in_dim.25.beta_ref
  5.9 98.8 %head.1 = (f32[1,128]{1,0:T(1,128)}, f32[1,128]{1,0:T(1,128)}, bf16[48,896]{1,0:T(8,128)(2,1)}, f32[2,896]{1,0:T(2,128)}, bf16[1536,4864]{1,0:T(8,128)(2,1)}, /*index=5*/bf16[1536,896]{1,0:T(8,128)(2,1)}) custom-call(bf16[48,896]{1,0:T(8,128)(2,1)} %hid_ref.1, f32[1,896]{1,0:T(1,128)} %broadcast_in_dim.24.gamma_ref, f32[1,896]{1,0:T(1,128)} %broadcast_in_dim.25.beta_ref, ...), custom_call_target="tpu_custom_call" | custom-call | tf_op jit(solution)/shard_map/head/pallas_call | solution.py:479
  104.7 22.4 %dembed.1 = f32[4864,896]{1,0:T(8,128)} custom-call(bf16[1536,896]{1,0:T(8,128)(2,1)} %get-tuple-element.15.x_ref, bf16[1536,4864]{1,0:T(8,128)(2,1)} %get-tuple-element.16.dz_ref), custom_call_target="tpu_custom_call" | custom-call | tf_op jit(solution)/shard_map/dembed/pallas_call | solution.py:541
  127.0 1.4 %slice_reduce_fusion = (f32[896]{0:T(1024)}, f32[896]{0:T(1024)}) fusion(f32[2,896]{1,0:T(2,128)} %get-tuple-element.17), kind=kLoop, calls=%fused_computation.2 | loop fusion | bytes 14336 | tf_op jit(solution)/shard_map/slice | solution.py:565
  128.4 1.1 slice_bitcast_fusion
  130.1 1.5 %copy.16 = bf16[48,896]{1,0:T(8,128)(2,1)} copy(bf16[48,896]{1,0:T(8,128)(2,1)} %get-tuple-element.28) | data formatting | bytes 172032
  (2 shorter events, 0.0 us)

commit v2 on v1

--- a/solution.py
+++ b/solution.py
@@ -28,9 +28,9 @@
 
 def head_kernel(
     side, tok, dim, vocab,
-    hid_ref, gamma_ref, beta_ref, aux_ref, bias_ref, emb_hbm,
+    hid_ref, gamma_ref, beta_ref, valid_ref, tgt_ref, mask_ref, emb_hbm,
     loss_ref, mean_ref, dhid_ref, dln_ref, dz_hbm, x_hbm,
-    emb, xbuf, z, tcol, stage, ms, ss, pk, lsec, wcol,
+    emb, xbuf, z, bias_ref, crow, tcol, stage, ms, ss, pk, lsec, wcol,
     st, rowa, rowb, mrow, lrow,
     dxt, rca, rcb, rcd, rcc, ga, gb, gpart,
     emb_sem, ag_s, ag_r, sa_s, sa_r, sb_s, sb_r,
@@ -82,9 +82,16 @@
         return cen * rstd, rstd
 
     xhat0, _ = normed()
-    xbuf[0, :, 0:dim] = (xhat0 * gamma_ref[...] + beta_ref[...]).astype(BF16)
-    xbuf[0, :, dim:wide] = aux_ref[...]
+    xbuf[0, :, 0:dim] = (xhat0 * gamma_ref[...][None, :] + beta_ref[...][None, :]).astype(BF16)
+    crow[...] = jnp.zeros((1, LANES), F32)
+    crow[0:1, 0:tok] = jnp.where(mask_ref[...] > 0, tgt_ref[...] + 1, 0).astype(F32)[None, :]
+    lane = lax.broadcasted_iota(jnp.int32, (tok, LANES), 1)
+    ccol = jnp.broadcast_to(crow[...], (LANES, LANES)).T[0:tok, :].astype(jnp.int32)
+    digits = jnp.where(lane == 0, ccol & 255, jnp.where(lane == 1, (ccol >> 8) & 255, (ccol >> 16) & 255))
+    xbuf[0, :, dim:wide] = jnp.where(lane < 3, digits, 0).astype(F32).astype(BF16)
     pl.semaphore_wait(barrier, len(row_peers) + side - 1)
+
+    bias_ref[...] = jnp.where(valid_ref[...] > 0, 0.0, -jnp.inf).astype(F32)[None, :]
 
     cut = 2 * tok // 3
     lo, hi = pl.ds(0, cut), pl.ds(cut, tok - cut)
@@ -164,7 +171,6 @@
             sb_op(t, dy).start()
 
     half = (vocab // LANES // 2) * LANES
-    lane = lax.broadcasted_iota(jnp.int32, (tok, LANES), 1)
     digit = jnp.where(lane == 0, 1.0, jnp.where(lane == 1, 256.0, jnp.where(lane == 2, 65536.0, 0.0)))
 
     def logits_tile(t, carry):
@@ -413,7 +419,7 @@
 
     dx = rcc[0] + rcc[1] + rcc[2] + rcc[3]
     xhat, rstd = normed()
-    g = dx * gamma_ref[...]
+    g = dx * gamma_ref[...][None, :]
     dh = rstd * (g - jnp.mean(g, axis=-1, keepdims=True) - xhat * jnp.mean(g * xhat, axis=-1, keepdims=True))
     gpart[0:1, :] = jnp.sum(dx * xhat, axis=0, keepdims=True)
     gpart[1:2, :] = jnp.sum(dx, axis=0, keepdims=True)
@@ -466,7 +472,7 @@
     dz_out(side - 1).wait()
 
 
-def head(mesh, hid, gamma, beta, aux, bias, emb):
+def head(mesh, hid, gamma, beta, valid, tgt, mask, emb):
     n_dev = mesh.shape["tp"]
     side = math.isqrt(n_dev // 2)
     tok, dim = hid.shape
@@ -486,12 +492,14 @@
             jax.ShapeDtypeStruct((seq, vocab), BF16),
             jax.ShapeDtypeStruct((seq, dim), BF16),
         ),
-        in_specs=[vmem] * 5 + [hbm],
+        in_specs=[vmem] * 6 + [hbm],
         out_specs=(vmem, vmem, vmem, vmem, hbm, hbm),
         scratch_shapes=[
             pltpu.VMEM((vocab, dim), BF16),
             pltpu.VMEM((n_dev, tok, dim + LANES), BF16),
             pltpu.VMEM((n_dev, tok, vocab), F32),
+            pltpu.VMEM((1, vocab), F32),
+            pltpu.VMEM((1, LANES), F32),
             pltpu.VMEM((n_dev, tok, LANES), jnp.int32),
             pltpu.VMEM((2, 8 * tok, vocab), BF16),
             pltpu.VMEM((8, tok, LANES), F32),
@@ -527,26 +535,35 @@
         compiler_params=pltpu.CompilerParams(
             collective_id=0, has_side_effects=True, vmem_limit_bytes=67043328),
         name="head",
-    )(hid, gamma, beta, aux, bias, emb)
-
-
-def dembed_kernel(x_ref, dz_ref, out_ref):
+    )(hid, gamma, beta, valid, tgt, mask, emb)
+
+
+def dembed_kernel(x_ref, dz_ref, loss_in, mean_in, dhid_in, dln_in, out_ref, loss_ref, mean_ref, dhid_ref, dln_ref):
     out_ref[...] = dot(dz_ref[...], x_ref[...], TN)
 
-
-def dembed(x, dz):
+    @pl.when(pl.program_id(0) == 0)
+    def _():
+        loss_ref[...] = loss_in[...]
+        mean_ref[...] = mean_in[...]
+        dhid_ref[...] = dhid_in[...]
+        dln_ref[...] = dln_in[...]
+
+
+def dembed(x, dz, loss, mean, dhid, dln):
     seq, dim = x.shape
     vocab = dz.shape[1]
     cols = 1664
+    small = [pl.BlockSpec(v.shape, lambda i: (0, 0)) for v in (loss, mean, dhid, dln)]
     return pl.pallas_call(
         dembed_kernel,
-        out_shape=jax.ShapeDtypeStruct((vocab, dim), F32),
+        out_shape=(jax.ShapeDtypeStruct((vocab, dim), F32),)
+        + tuple(jax.ShapeDtypeStruct(v.shape, v.dtype) for v in (loss, mean, dhid, dln)),
         grid=(pl.cdiv(vocab, cols),),
-        in_specs=[pl.BlockSpec((seq, dim), lambda i: (0, 0)), pl.BlockSpec((seq, cols), lambda i: (0, i))],
-        out_specs=pl.BlockSpec((cols, dim), lambda i: (i, 0)),
+        in_specs=[pl.BlockSpec((seq, dim), lambda i: (0, 0)), pl.BlockSpec((seq, cols), lambda i: (0, i))] + small,
+        out_specs=tuple([pl.BlockSpec((cols, dim), lambda i: (i, 0))] + small),
         compiler_params=pltpu.CompilerParams(vmem_limit_bytes=67043328),
         name="dembed",
-    )(x, dz)
+    )(x, dz, loss, mean, dhid, dln)
 
 
 def solution(mesh):
@@ -554,15 +571,10 @@
     row_spec = P(("dp", "tp"), None)
 
     def local_step(hidden_blk, ln_gamma, ln_beta, embed_blk, valid_blk, tgt_blk, mask_blk):
-        tok = hidden_blk.shape[0]
-        code = jnp.where(mask_blk > 0, tgt_blk + 1, 0)
-        lane = lax.broadcasted_iota(jnp.int32, (tok, LANES), 1)
-        aux = jnp.where(lane < 3, (code[:, None] >> (8 * jnp.minimum(lane, 2))) & 255, 0).astype(BF16)
-        bias = jnp.where(valid_blk > 0, 0.0, -jnp.inf).astype(F32)[None, :]
         loss, mean, dhid, dln, dz, x = head(
-            mesh, hidden_blk, ln_gamma[None, :], ln_beta[None, :], aux, bias, embed_blk)
-        d_embed = dembed(x, dz)
-        return loss[0, :tok], mean[0, :1], dhid, d_embed, dln[0], dln[1]
+            mesh, hidden_blk, ln_gamma, ln_beta, valid_blk, tgt_blk, mask_blk, embed_blk)
+        d_embed, loss, mean, d_hidden, dln = dembed(x, dz, loss, mean, dhid, dln)
+        return loss[0, :dhid.shape[0]], mean[0, :1], d_hidden, d_embed, dln[0], dln[1]
 
     return jax.shard_map(
         local_step, mesh=mesh,

time: 133 us -> 125 us (0.940)
  local copies, waits for them, and re-layouts: 7.19 us -> 2.55 us
  other arithmetic: 2.09 us -> 0 us
  between operations: 2.34 us -> 0.64 us
    broadcast_in_dim x3 -> x0, local copies, waits for them, and re-layouts: 3.15 us -> none  [the longest x1 1.27 us: local_step(): ln_gamma[None, :]]
    unnamed x1 -> x0, local copies, waits for them, and re-layouts: 1.53 us -> none
    select_n x2 -> x0, other arithmetic: 1.41 us -> none  [the longest x1 0.73 us: local_step(): bias = jnp.where(valid_blk > 0, 0.0, -jnp.inf).astype(F32)[None, :]]
where the time goes in v2:
time: 125 us
  Pallas kernels  122 us (98%)
  local copies, waits for them, and re-layouts  2.55 us (2%)
    pallas_call x1, Pallas kernels, head(): pl.pallas_call(functools.partial(head_kernel, side, tok, dim, vocab), out...  99.2 us
    pallas_call x1, Pallas kernels, dembed(): pl.pallas_call(dembed_kernel, out_shape=(jax.ShapeDtypeStruct((vocab, dim...  22.5 us

profile of v2, /device:TPU:97, one launch (start us, length us, event | category | flops | bytes accessed | tf_op | source)
XLA Modules:
  0.0 124.9 jit_solution(143009247520930079)
XLA Ops:
  0.6 99.2 %head.1 = (f32[1,128]{1,0:T(1,128)}, f32[1,128]{1,0:T(1,128)}, bf16[48,896]{1,0:T(8,128)(2,1)}, f32[2,896]{1,0:T(2,128)}, bf16[1536,4864]{1,0:T(8,128)(2,1)}, /*index=5*/bf16[1536,896]{1,0:T(8,128)(2,1)}) custom-call(bf16[48,896]{1,0:T(8,128)(2,1)} %hid_ref.1, f32[896]{0:T(1024)} %gamma_ref.1, f32[896]{0:T(1024)} %beta_ref.1, s32[4864]{0:T(1024)} %valid_ref.1, ...), custom_call_target="tpu_custom_call" | custom-call | tf_op jit(solution)/shard_map/head/pallas_call | solution.py:485
  99.8 22.5 %dembed.1 = (f32[4864,896]{1,0:T(8,128)}, f32[1,128]{1,0:T(1,128)}, f32[1,128]{1,0:T(1,128)}, bf16[48,896]{1,0:T(8,128)(2,1)}, f32[2,896]{1,0:T(2,128)}) custom-call(bf16[1536,896]{1,0:T(8,128)(2,1)} %get-tuple-element.17.x_ref, bf16[1536,4864]{1,0:T(8,128)(2,1)} %get-tuple-element.18.dz_ref, f32[1,128]{1,0:T(1,128)} %get-tuple-element.19.loss_in, ...), custom_call_target="tpu_custom_call" | custom-call | tf_op jit(solution)/shard_map/dembed/pallas_call | solution.py:557
  122.3 1.2 slice_bitcast_fusion
  123.5 1.4 %slice_reduce_fusion = (f32[896]{0:T(1024)}, f32[896]{0:T(1024)}) fusion(f32[2,896]{1,0:T(2,128)} %get-tuple-element.27), kind=kLoop, calls=%fused_computation | loop fusion | bytes 14336 | tf_op jit(solution)/shard_map/slice | solution.py:577

commit v3 on v2

--- a/solution.py
+++ b/solution.py
@@ -29,7 +29,7 @@
 def head_kernel(
     side, tok, dim, vocab,
     hid_ref, gamma_ref, beta_ref, valid_ref, tgt_ref, mask_ref, emb_hbm,
-    loss_ref, mean_ref, dhid_ref, dln_ref, dz_hbm, x_hbm,
+    loss_ref, mean_ref, dhid_ref, dgam_ref, dbet_ref, dz_hbm, x_hbm,
     emb, xbuf, z, bias_ref, crow, tcol, stage, ms, ss, pk, lsec, wcol,
     st, rowa, rowb, mrow, lrow,
     dxt, rca, rcb, rcd, rcc, ga, gb, gpart,
@@ -444,7 +444,9 @@
     for dy in range(1, side):
         ref = gb.at[wrap(y - dy)]
         remote(ref, ref, gb_s.at[dy], gb_r.at[dy], partner).wait_recv()
-    dln_ref[...] = functools.reduce(jnp.add, [gb[i] for i in range(side)])
+    dln = functools.reduce(jnp.add, [gb[i] for i in range(side)])
+    dgam_ref[...] = dln[0:1, :]
+    dbet_ref[...] = dln[1:2, :]
 
     for k in sorted(ag_ops):
         ag_ops[k].wait_send()
@@ -488,12 +490,13 @@
             jax.ShapeDtypeStruct((1, LANES), F32),
             jax.ShapeDtypeStruct((1, LANES), F32),
             jax.ShapeDtypeStruct((tok, dim), BF16),
-            jax.ShapeDtypeStruct((2, dim), F32),
+            jax.ShapeDtypeStruct((1, dim), F32),
+            jax.ShapeDtypeStruct((1, dim), F32),
             jax.ShapeDtypeStruct((seq, vocab), BF16),
             jax.ShapeDtypeStruct((seq, dim), BF16),
         ),
         in_specs=[vmem] * 6 + [hbm],
-        out_specs=(vmem, vmem, vmem, vmem, hbm, hbm),
+        out_specs=(vmem, vmem, vmem, vmem, vmem, hbm, hbm),
         scratch_shapes=[
             pltpu.VMEM((vocab, dim), BF16),
             pltpu.VMEM((n_dev, tok, dim + LANES), BF16),
@@ -538,7 +541,10 @@
     )(hid, gamma, beta, valid, tgt, mask, emb)
 
 
-def dembed_kernel(x_ref, dz_ref, loss_in, mean_in, dhid_in, dln_in, out_ref, loss_ref, mean_ref, dhid_ref, dln_ref):
+def dembed_kernel(
+    x_ref, dz_ref, loss_in, mean_in, dhid_in, dgam_in, dbet_in,
+    out_ref, loss_ref, mean_ref, dhid_ref, dgam_ref, dbet_ref,
+):
     out_ref[...] = dot(dz_ref[...], x_ref[...], TN)
 
     @pl.when(pl.program_id(0) == 0)
@@ -546,24 +552,27 @@
         loss_ref[...] = loss_in[...]
         mean_ref[...] = mean_in[...]
         dhid_ref[...] = dhid_in[...]
-        dln_ref[...] = dln_in[...]
-
-
-def dembed(x, dz, loss, mean, dhid, dln):
+        dgam_ref[...] = dgam_in[0, :]
+        dbet_ref[...] = dbet_in[0, :]
+
+
+def dembed(x, dz, loss, mean, dhid, dgam, dbet):
     seq, dim = x.shape
     vocab = dz.shape[1]
     cols = 1664
-    small = [pl.BlockSpec(v.shape, lambda i: (0, 0)) for v in (loss, mean, dhid, dln)]
+    small = [pl.BlockSpec(v.shape, lambda i: (0, 0)) for v in (loss, mean, dhid, dgam, dbet)]
+    flat = pl.BlockSpec((dim,), lambda i: (0,))
     return pl.pallas_call(
         dembed_kernel,
         out_shape=(jax.ShapeDtypeStruct((vocab, dim), F32),)
-        + tuple(jax.ShapeDtypeStruct(v.shape, v.dtype) for v in (loss, mean, dhid, dln)),
+        + tuple(jax.ShapeDtypeStruct(v.shape, v.dtype) for v in (loss, mean, dhid))
+        + (jax.ShapeDtypeStruct((dim,), F32),) * 2,
         grid=(pl.cdiv(vocab, cols),),
         in_specs=[pl.BlockSpec((seq, dim), lambda i: (0, 0)), pl.BlockSpec((seq, cols), lambda i: (0, i))] + small,
-        out_specs=tuple([pl.BlockSpec((cols, dim), lambda i: (i, 0))] + small),
+        out_specs=tuple([pl.BlockSpec((cols, dim), lambda i: (i, 0))] + small[:3] + [flat] * 2),
         compiler_params=pltpu.CompilerParams(vmem_limit_bytes=67043328),
         name="dembed",
-    )(x, dz, loss, mean, dhid, dln)
+    )(x, dz, loss, mean, dhid, dgam, dbet)
 
 
 def solution(mesh):
@@ -571,10 +580,10 @@
     row_spec = P(("dp", "tp"), None)
 
     def local_step(hidden_blk, ln_gamma, ln_beta, embed_blk, valid_blk, tgt_blk, mask_blk):
-        loss, mean, dhid, dln, dz, x = head(
+        loss, mean, dhid, dgam, dbet, dz, x = head(
             mesh, hidden_blk, ln_gamma, ln_beta, valid_blk, tgt_blk, mask_blk, embed_blk)
-        d_embed, loss, mean, d_hidden, dln = dembed(x, dz, loss, mean, dhid, dln)
-        return loss[0, :dhid.shape[0]], mean[0, :1], d_hidden, d_embed, dln[0], dln[1]
+        d_embed, loss, mean, d_hidden, d_gamma, d_beta = dembed(x, dz, loss, mean, dhid, dgam, dbet)
+        return loss[0, :dhid.shape[0]], mean[0, :1], d_hidden, d_embed, d_gamma, d_beta
 
     return jax.shard_map(
         local_step, mesh=mesh,

time: 125 us -> 124 us (level)
  local copies, waits for them, and re-layouts: 2.55 us -> 1.17 us
    slice x1 -> x0, local copies, waits for them, and re-layouts: 1.39 us -> none  [local_step(): dln[1]]
where the time goes in v3:
time: 124 us; the launch traced here: 123 us
  Pallas kernels  122 us (98%)
    pallas_call x1, Pallas kernels, head(): pl.pallas_call(functools.partial(head_kernel, side, tok, dim, vocab), out...  99.2 us
    pallas_call x1, Pallas kernels, dembed(): pl.pallas_call(dembed_kernel, out_shape=(jax.ShapeDtypeStruct((vocab, dim...  22.5 us

profile of v3, /device:TPU:97, one launch (start us, length us, event | category | flops | bytes accessed | tf_op | source)
XLA Modules:
  0.0 123.5 jit_solution(10498355648318635937)
XLA Ops:
  0.6 99.2 %head.1 = (f32[1,128]{1,0:T(1,128)}, f32[1,128]{1,0:T(1,128)}, bf16[48,896]{1,0:T(8,128)(2,1)}, f32[1,896]{1,0:T(1,128)}, f32[1,896]{1,0:T(1,128)}, /*index=5*/b...) custom-call(bf16[48,896]{1,0:T(8,128)(2,1)} %hid_ref.1, f32[896]{0:T(1024)} %gamma_ref.1, f32[896]{0:T(1024)} %beta_ref.1, ...), custom_call_target="tpu_custom_call" | custom-call | tf_op jit(solution)/shard_map/head/pallas_call | solution.py:487
  99.8 22.5 %dembed.1 = (f32[4864,896]{1,0:T(8,128)}, f32[1,128]{1,0:T(1,128)}, f32[1,128]{1,0:T(1,128)}, bf16[48,896]{1,0:T(8,128)(2,1)}, f32[896]{0:T(1024)}, /*index=5*/f32[896]{0:T(1024)}) custom-call(bf16[1536,896]{1,0:T(8,128)(2,1)} %get-tuple-element.19.x_ref, bf16[1536,4864]{1,0:T(8,128)(2,1)} %get-tuple-element.20.dz_ref, f32[1,128]{1,0:T(1,128)} %get-tuple-element.21.loss_in, ...), custom_call_target="tpu_custom_call" | custom-call | tf_op jit(solution)/shard_map/dembed/pallas_call | solution.py:565
  122.3 1.2 slice_bitcast_fusion
